TPU v7x, 32 devices: a whole 2x2x4 slice. The times are simulated.
32 devices in a mesh: dp: 8 (over z, y), rep: 4 (over x, core).
Axes of the slice: x: 2, y: 2, z: 4, core: 2. Of those that a mesh axis runs over, the one named last changes fastest.
Arguments:
- enc: bfloat16 [64, 48, 640], P(('dp', 'rep')), may hold values from -6 to 6
- pred: bfloat16 [64, 17, 640], P(('dp', 'rep')), may hold values from -6 to 6
- labels: int32 [64, 16], P(('dp', 'rep')), may hold values from 1 to 4095
- frame_len: int32 [64], P(('dp', 'rep')), may hold values from 24 to 48, as said below
- label_len: int32 [64], P(('dp', 'rep')), may hold values from 1 to 16, as said below
- w_enc: bfloat16 [640, 640], replicated, may hold values from -0.25 to 0.25
- w_pred: bfloat16 [640, 640], replicated, may hold values from -0.25 to 0.25
- b_joint: bfloat16 [640], replicated, may hold values from -3 to 3
- w_out: bfloat16 [640, 4096], replicated, may hold values from -0.69921875 to 0.69921875
- b_out: bfloat16 [4096], replicated, may hold values from -5 to 5
Outputs:
- step_enc: float32 [640, 640], replicated
- step_pred: float32 [640, 640], replicated
- step_out: float32 [640, 4096], replicated
- step_bias_out: float32 [4096], replicated
- step_bias_joint: float32 [640], replicated
- mean_loss: float32 [], replicated
Inputs may be any that keep to these rules, and one draw needn't show every extreme that they name: `frame_len`: the last utterance has all 48 frames. `label_len`: the last utterance has all 16 labels.
All inputs are finite; a program needn't handle non-finite values.
Results may differ from a plain program's by a relative error of at most 0.0055.
Values sent between devices are 32-bit elements; how exact they have to be, the bound alone decides.
No kernel may reach another device: no remote copies, remote signals or barrier semaphores. Data moves between devices by JAX's collectives and lax.ppermute only.
A program may use at most 256 MiB of HBM per device.

v0:
```python
import jax
import jax.numpy as jnp
from jax import lax
from jax.sharding import PartitionSpec as P

NEG = -1e30
EPS = 1e-06


def diagonal_index(num_frames, count_labels):
    diagonals = jnp.arange(num_frames + count_labels - 1, dtype=jnp.int32)
    positions = jnp.arange(count_labels, dtype=jnp.int32)
    return diagonals[:, None] - positions[None, :]


def skewed(grid):
    utterances, num_frames, count_labels = grid.shape
    positions = jnp.arange(count_labels, dtype=jnp.int32)
    frame_index = diagonal_index(num_frames, count_labels)
    inside = (frame_index >= 0) & (frame_index < num_frames)
    picked = grid[:, jnp.clip(frame_index, 0, num_frames - 1), positions[None, :]]
    picked = jnp.where(inside[None, :, :], picked, NEG)
    return jnp.transpose(picked, (1, 0, 2))


def unskewed(diag_grid, num_frames):
    count_labels = diag_grid.shape[2]
    by_utterance = jnp.transpose(diag_grid, (1, 0, 2))
    frame_ids = jnp.arange(num_frames, dtype=jnp.int32)
    positions = jnp.arange(count_labels, dtype=jnp.int32)
    return by_utterance[:, frame_ids[:, None] + positions[None, :], positions[None, :]]


def lattice(blank, emit, frame_len, label_len):
    utterances, num_frames, count_labels = blank.shape
    positions = jnp.arange(count_labels, dtype=jnp.int32)
    frame_index = diagonal_index(num_frames, count_labels)
    blank_diag = skewed(blank)
    emit_diag = skewed(emit)
    neg_block = jnp.full((1, utterances, count_labels), NEG, jnp.float32)
    neg_col = jnp.full((utterances, 1), NEG, jnp.float32)
    neg_grid = jnp.full((utterances, count_labels), NEG, jnp.float32)
    frame_count = frame_len[:, None]
    label_count = label_len[:, None]
    terminal = jnp.where(positions[None, :] == label_count, 0.0, NEG).astype(jnp.float32)
    first_diag = jnp.broadcast_to(
        jnp.where(positions == 0, 0.0, NEG).astype(jnp.float32)[None, :], (utterances, count_labels)
    )
    blank_prev = jnp.concatenate([neg_block, blank_diag[:-1]], axis=0)
    emit_prev = jnp.concatenate([neg_block, emit_diag[:-1]], axis=0)
    steps_total = frame_index.shape[0]
    step_ids = jnp.arange(steps_total, dtype=jnp.int32)

    def both_ways(carry, inputs):
        alpha_prev, beta_next = carry
        step_id, blank_fwd, emit_fwd, frames_fwd, blank_back, emit_back, frames_back = inputs
        top_term = alpha_prev + blank_fwd
        left_term = jnp.concatenate([neg_col, (alpha_prev + emit_fwd)[:, :-1]], axis=1)
        alpha_cell = jnp.logaddexp(top_term, left_term)
        inside = (frames_fwd >= 0) & (frames_fwd < num_frames)
        alpha_cell = jnp.where(inside[None, :], alpha_cell, NEG)
        alpha_cell = jnp.where(step_id == 0, first_diag, alpha_cell)
        frames_row = frames_back[None, :]
        below = jnp.where(
            frames_row == frame_count - 1,
            terminal,
            jnp.where(frames_row >= frame_count, neg_grid, beta_next),
        )
        right_term = jnp.concatenate([beta_next[:, 1:], neg_col], axis=1)
        beta_cell = jnp.logaddexp(below + blank_back, right_term + emit_back)
        live = (positions[None, :] <= label_count) & (frames_row < frame_count) & (frames_row >= 0)
        beta_cell = jnp.where(live, beta_cell, NEG)
        return ((alpha_cell, beta_cell), (alpha_cell, beta_cell, below))

    inputs = (
        step_ids,
        blank_prev,
        emit_prev,
        frame_index,
        jnp.flip(blank_diag, 0),
        jnp.flip(emit_diag, 0),
        jnp.flip(frame_index, 0),
    )
    unused_last, (alpha_diag, beta_rev, below_rev) = lax.scan(
        both_ways, (first_diag, neg_grid), inputs
    )
    alpha = unskewed(alpha_diag, num_frames)
    beta = unskewed(jnp.flip(beta_rev, 0), num_frames)
    below = unskewed(jnp.flip(below_rev, 0), num_frames)
    return (alpha, beta, below)


def joint_forward(enc_row, pred_row, label_row, w_enc, w_pred, b_joint, w_out, b_out):
    num_frames = enc_row.shape[0]
    count_labels = pred_row.shape[0]
    joint_width = w_enc.shape[1]
    vocab_size = w_out.shape[1]
    enc_proj = jnp.dot(enc_row, w_enc, preferred_element_type=jnp.float32)
    pred_proj = jnp.dot(pred_row, w_pred, preferred_element_type=jnp.float32) + b_joint.astype(
        jnp.float32
    )
    hidden = jnp.tanh(enc_proj[:, None, :] + pred_proj[None, :, :]).astype(jnp.bfloat16)
    hidden = lax.optimization_barrier(hidden.reshape(num_frames * count_labels, joint_width))
    logits = jnp.dot(hidden, w_out, preferred_element_type=jnp.float32) + b_out.astype(jnp.float32)
    log_probs = jax.nn.log_softmax(logits, axis=-1)
    targets = jnp.concatenate([label_row, jnp.ones((1,), jnp.int32)])
    target_cols = jnp.tile(targets, num_frames)
    vocab_pos = jnp.arange(vocab_size, dtype=jnp.int32)
    is_target = vocab_pos[None, :] == target_cols[:, None]
    emit = jnp.sum(jnp.where(is_target, log_probs, 0.0), axis=1).reshape(num_frames, count_labels)
    blank = log_probs[:, 0].reshape(num_frames, count_labels)
    return (hidden, log_probs, blank, emit)


def joint_backward(
    enc_row, pred_row, label_row, hidden, log_probs, blank, emit, alpha, beta, below, w_out
):
    num_frames = enc_row.shape[0]
    count_labels = pred_row.shape[0]
    joint_width = hidden.shape[1]
    vocab_size = w_out.shape[1]
    targets = jnp.concatenate([label_row, jnp.ones((1,), jnp.int32)])
    target_cols = jnp.tile(targets, num_frames)
    vocab_pos = jnp.arange(vocab_size, dtype=jnp.int32)
    is_target = vocab_pos[None, :] == target_cols[:, None]
    log_total = beta[0, 0]
    right = jnp.concatenate([beta[:, 1:], jnp.full((num_frames, 1), NEG, jnp.float32)], axis=1)
    blank_occ = jnp.exp(alpha + blank + below - log_total).reshape(-1)
    emit_occ = jnp.exp(alpha + emit + right - log_total).reshape(-1)
    probs = jnp.exp(log_probs)
    grad_logits = probs * (blank_occ + emit_occ)[:, None]
    grad_logits = grad_logits - jnp.where(vocab_pos[None, :] == 0, blank_occ[:, None], 0.0)
    grad_logits = grad_logits - jnp.where(is_target, emit_occ[:, None], 0.0)
    grad_logits = lax.optimization_barrier(grad_logits.astype(jnp.bfloat16))
    grad_out = lax.dot_general(
        hidden, grad_logits, (((0,), (0,)), ((), ())), preferred_element_type=jnp.float32
    )
    grad_bias_out = jnp.sum(grad_logits.astype(jnp.float32), axis=0)
    grad_hidden = lax.dot_general(
        grad_logits, w_out, (((1,), (1,)), ((), ())), preferred_element_type=jnp.float32
    )
    hidden_wide = hidden.astype(jnp.float32)
    grad_pre = (grad_hidden * (1.0 - hidden_wide * hidden_wide)).reshape(
        num_frames, count_labels, joint_width
    )
    grad_enc_proj = lax.optimization_barrier(jnp.sum(grad_pre, axis=1).astype(jnp.bfloat16))
    grad_pred_proj = lax.optimization_barrier(jnp.sum(grad_pre, axis=0).astype(jnp.bfloat16))
    grad_enc = lax.dot_general(
        enc_row, grad_enc_proj, (((0,), (0,)), ((), ())), preferred_element_type=jnp.float32
    )
    grad_pred = lax.dot_general(
        pred_row, grad_pred_proj, (((0,), (0,)), ((), ())), preferred_element_type=jnp.float32
    )
    grad_bias_joint = jnp.sum(grad_pred_proj.astype(jnp.float32), axis=0)
    return (-log_total, (grad_enc, grad_pred, grad_out, grad_bias_out, grad_bias_joint))


def local_sums(enc, pred, labels, frame_len, label_len, w_enc, w_pred, b_joint, w_out, b_out):

    def forward_one(unused_carry, inputs):
        enc_row, pred_row, label_row = inputs
        return (
            None,
            joint_forward(enc_row, pred_row, label_row, w_enc, w_pred, b_joint, w_out, b_out),
        )

    unused_none, (hidden, log_probs, blank, emit) = lax.scan(forward_one, None, (enc, pred, labels))
    alpha, beta, below = lattice(blank, emit, frame_len, label_len)
    initial = (
        jnp.zeros(w_enc.shape, jnp.float32),
        jnp.zeros(w_pred.shape, jnp.float32),
        jnp.zeros(w_out.shape, jnp.float32),
        jnp.zeros(b_out.shape, jnp.float32),
        jnp.zeros(b_joint.shape, jnp.float32),
    )

    def backward_one(carry, inputs):
        loss_sum, grad_sums = carry
        loss_one, grads_one = joint_backward(*inputs, w_out)
        added = tuple((total + term for total, term in zip(grad_sums, grads_one)))
        return ((loss_sum + loss_one, added), None)

    (loss_sum, grads), unused_ys = lax.scan(
        backward_one,
        (jnp.float32(0.0), initial),
        (enc, pred, labels, hidden, log_probs, blank, emit, alpha, beta, below),
    )
    return (loss_sum, grads)


def squares(items):
    total_sq = jnp.float32(0.0)
    for item in items:
        total_sq = total_sq + jnp.sum(item * item)
    return total_sq


def per_device(enc, pred, labels, frame_len, label_len, w_enc, w_pred, b_joint, w_out, b_out):
    loss_local, grads = local_sums(
        enc, pred, labels, frame_len, label_len, w_enc, w_pred, b_joint, w_out, b_out
    )
    count_local = jnp.sum(label_len).astype(jnp.float32)
    param_count = jnp.float32(w_enc.size + w_pred.size + w_out.size + b_out.size + b_joint.size)
    loss_total, label_total = lax.psum((loss_local, count_local), ("dp", "rep"))
    summed = lax.psum((grads[0], grads[1], grads[2], grads[3], grads[4]), ("dp", "rep"))
    scale = lax.rsqrt(squares(summed) / param_count + EPS)
    result = tuple((item * scale for item in summed))
    return (result[0], result[1], result[2], result[3], result[4], loss_total / label_total)


def solution(mesh):
    in_specs = (
        P(("dp", "rep"), None, None),
        P(("dp", "rep"), None, None),
        P(("dp", "rep"), None),
        P(("dp", "rep")),
        P(("dp", "rep")),
        P(),
        P(),
        P(),
        P(),
        P(),
    )
    out_specs = (P(), P(), P(), P(), P(), P())
    return jax.shard_map(
        per_device, mesh=mesh, in_specs=in_specs, out_specs=out_specs, check_vma=False
    )
```

profile of v0, /device:TPU:0, one launch (start us, length us, event | category | flops | bytes accessed | tf_op | source)
XLA Modules:
  0.0 639.8 jit_solution(4801691328892887368)
XLA Ops:
  11.1 88.6 %while.58 = (s32[]{:T(128)}, bf16[2,816,640]{2,1,0:T(8,128)(2,1)}, f32[2,816,4096]{2,1,0:T(8,128)}, f32[2,48,17]{2,1,0:T(8,128)S(1)}, f32[2,48,17]{2,1,0:T(8,128...) while((s32[]{:T(128)}, bf16[2,816,640]{2,1,0:T(8,128)(2,1)}, ...), condition=%wide.region_4.5_spmd, body=%wide.region_0.4_spmd.sunk | while | flops 4369261056 | bytes 147507888 | solution.py:167
  16.4 7.5 %add_reduce_fusion.2 = (f32[816]{0:T(1024)S(1)}, f32[816,4096]{1,0:T(8,128)S(1)}) fusion(f32[4096]{0:T(1024)S(1)} %convert_element_type.65, bf16[816,640]{1,0:T(8,128)(2,1)S(1)} %convert_element_type.64, bf16[640,4096]{1,0:T(8,128)(2,1)} %get-tuple-element.1143), kind=kOutput, calls=%fused_computation.66.clone.1 | convolution fusion | flops 4284873984 | bytes 19676352 | tf_op jit(solution)/shard_map/while/body/eval_jaxpr/dot_general | solution.py:104
  28.9 12.7 %select_reduce_fusion.2 = (f32[816]{0:T(1024)S(1)}, f32[816,4096]{1,0:T(8,128)}) fusion(s32[816]{0:T(1024)S(1)} %eq.178, f32[816]{0:T(1024)S(1)} %log.11, f32[816]{0:T(1024)S(1)} %get-tuple-element.1053, f32[816,4096]{1,0:T(8,128)} %copy-done.1, f32[4096]{0:T(1024)S(1)} %convert_element_type.65), kind=kLoop, calls=%fused_computation.62.clone.1 | loop fusion | flops 20053200 | bytes 26768128 | tf_op jit(solution)/shard_map/while/body/eval_jaxpr/reduce_sum | solution.py:110
  43.1 11.3 %bitcast_dynamic-update-slice_fusion.5 = f32[2,816,4096]{2,1,0:T(8,128)} fusion(f32[2,816,4096]{2,1,0:T(8,128)} %get-tuple-element.1120, s32[]{:T(128)} %get-tuple-element.1118, f32[816,4096]{1,0:T(8,128)} %get-tuple-element.1054), kind=kLoop, calls=%fused_computation.61.clone.1 | loop fusion | bytes 26739200 | tf_op jit(solution)/shard_map/while/body/jit(dynamic_update_index_in_dim)/dynamic_update_slice | solution.py:167
  60.6 7.5 %add_reduce_fusion.2 = (f32[816]{0:T(1024)S(1)}, f32[816,4096]{1,0:T(8,128)S(1)}) fusion(f32[4096]{0:T(1024)S(1)} %convert_element_type.65, bf16[816,640]{1,0:T(8,128)(2,1)S(1)} %convert_element_type.64, bf16[640,4096]{1,0:T(8,128)(2,1)} %get-tuple-element.1143), kind=kOutput, calls=%fused_computation.66.clone.1 | convolution fusion | flops 4284873984 | bytes 19676352 | tf_op jit(solution)/shard_map/while/body/eval_jaxpr/dot_general | solution.py:104
  73.2 12.7 %select_reduce_fusion.2 = (f32[816]{0:T(1024)S(1)}, f32[816,4096]{1,0:T(8,128)}) fusion(s32[816]{0:T(1024)S(1)} %eq.178, f32[816]{0:T(1024)S(1)} %log.11, f32[816]{0:T(1024)S(1)} %get-tuple-element.1053, f32[816,4096]{1,0:T(8,128)} %copy-done.1, f32[4096]{0:T(1024)S(1)} %convert_element_type.65), kind=kLoop, calls=%fused_computation.62.clone.1 | loop fusion | flops 20053200 | bytes 26768128 | tf_op jit(solution)/shard_map/while/body/eval_jaxpr/reduce_sum | solution.py:110
  87.3 11.3 %bitcast_dynamic-update-slice_fusion.5 = f32[2,816,4096]{2,1,0:T(8,128)} fusion(f32[2,816,4096]{2,1,0:T(8,128)} %get-tuple-element.1120, s32[]{:T(128)} %get-tuple-element.1118, f32[816,4096]{1,0:T(8,128)} %get-tuple-element.1054), kind=kLoop, calls=%fused_computation.61.clone.1 | loop fusion | bytes 26739200 | tf_op jit(solution)/shard_map/while/body/jit(dynamic_update_index_in_dim)/dynamic_update_slice | solution.py:167
  100.8 12.3 %gather_fusion = f32[1088,2]{1,0:T(8,128)S(1)} fusion(f32[2,48,17]{0,1,2:T(8,128)S(1)} %copy.55, s32[1088]{0:T(1024)S(1)} %reshape.180), kind=kCustom, calls=%fused_computation | custom fusion | bytes 26112 | tf_op jit(solution)/shard_map/gather | solution.py:21
  113.6 12.1 %gather_fusion.1 = f32[1088,2]{1,0:T(8,128)S(1)} fusion(f32[2,48,17]{0,1,2:T(8,128)S(1)} %copy.57, s32[1088]{0:T(1024)S(1)} %reshape.180), kind=kCustom, calls=%fused_computation.1 | custom fusion | bytes 26112 | tf_op jit(solution)/shard_map/gather | solution.py:21
  126.3 106.5 %while.59 = (s32[]{:T(128)}, f32[2,17]{1,0:T(2,128)S(1)}, f32[2,17]{1,0:T(2,128)S(1)}, f32[64,2,17]{2,1,0:T(2,128)S(1)}, f32[64,2,17]{2,1,0:T(2,128)S(1)}, /*ind...) while((s32[]{:T(128)}, f32[2,17]{1,0:T(2,128)S(1)}, ...), condition=%wide.region_6.7_spmd.clone, body=%wide.region_5.6_spmd.clone.sunk | while | flops 1434 | bytes 22799 | solution.py:84
  233.9 9.8 %gather_fusion.2 = f32[816,2]{1,0:T(8,128)S(1)} fusion(f32[2,64,17]{0,1,2:T(8,128)S(1)} %bitcast.183, s32[816]{0:T(1024)S(1)} %reshape.192), kind=kCustom, calls=%fused_computation.2 | custom fusion | bytes 19584 | tf_op jit(solution)/shard_map/gather | solution.py:31
  245.2 10.0 %gather_fusion.4 = f32[816,2]{1,0:T(8,128)S(1)} fusion(f32[2,64,17]{0,1,2:T(8,128)S(1)} %bitcast.185, s32[816]{0:T(1024)S(1)} %reshape.192), kind=kCustom, calls=%fused_computation.4 | custom fusion | bytes 19584 | tf_op jit(solution)/shard_map/gather | solution.py:31
  256.3 9.8 %gather_fusion.3 = f32[816,2]{1,0:T(8,128)S(1)} fusion(f32[2,64,17]{0,1,2:T(8,128)S(1)} %bitcast.184, s32[816]{0:T(1024)S(1)} %reshape.192), kind=kCustom, calls=%fused_computation.3 | custom fusion | bytes 19584 | tf_op jit(solution)/shard_map/gather | solution.py:31
  266.5 91.0 %while.60 = (s32[]{:T(128)}, f32[]{:T(128)}, f32[640,640]{1,0:T(8,128)}, f32[640,640]{1,0:T(8,128)}, f32[640,4096]{1,0:T(8,128)}, /*index=5*/f32[4096]{0:T(1024)...) while((s32[]{:T(128)}, f32[]{:T(128)}, ...), condition=%wide.region_12.13_spmd.clone, body=%wide.region_7.12_spmd.clone.sunk | while | flops 8649718784 | bytes 146314000 | solution.py:183
  269.0 11.2 %fusion.89 = bf16[816,4096]{1,0:T(8,128)(2,1)} fusion(f32[2,816,4096]{2,1,0:T(8,128)} %get-tuple-element.1259, s32[]{:T(128)} %get-tuple-element.1229, f32[816]{0:T(1024)S(1)} %reshape.215, s32[816]{0:T(1024)S(1)} %eq.189, f32[816]{0:T(1024)S(1)} %exp.63, f32[816]{0:T(1024)S(1)} %add.404, pred[4096]{0:T(1024)(128)(4,1)S(1)} %iota_compare_fusion.4), kind=kLoop, calls=%fused_computation.33.clone.1 | loop fusion | flops 23396352 | bytes 20071172 | tf_op jit(solution)/shard_map/while/body/eval_jaxpr/convert_element_type | solution.py:134
  280.2 10.6 %select_add_fusion.12 = f32[640,4096]{1,0:T(8,128)} fusion(f32[640,4096]{1,0:T(8,128)} %get-tuple-element.1233, bf16[816,4096]{1,0:T(8,128)(2,1)} %fusion.89, pred[]{:T(512)S(6)} %compare.12, bf16[2,816,640]{2,1,0:T(8,128)(2,1)} %get-tuple-element.1266, s32[]{:T(128)} %get-tuple-element.1229), kind=kOutput, calls=%fused_computation.36.clone.1 | convolution fusion | flops 4283432960 | bytes 28701184 | tf_op jit(solution)/shard_map/while/body/eval_jaxpr/dot_general | solution.py:135
  290.8 8.1 %subtract_multiply_fusion.2 = f32[816,640]{1,0:T(8,128)} fusion(bf16[816,4096]{1,0:T(8,128)(2,1)S(1)} %copy-done, bf16[640,4096]{1,0:T(8,128)(2,1)S(1)} %bitcast.202, bf16[2,816,640]{2,1,0:T(8,128)(2,1)} %get-tuple-element.1266, s32[]{:T(128)} %get-tuple-element.1229), kind=kOutput, calls=%fused_computation.37.clone.1 | convolution fusion | flops 4280279040 | bytes 15060996 | tf_op jit(solution)/shard_map/while/body/eval_jaxpr/dot_general | solution.py:139
  312.2 11.2 %fusion.89 = bf16[816,4096]{1,0:T(8,128)(2,1)} fusion(f32[2,816,4096]{2,1,0:T(8,128)} %get-tuple-element.1259, s32[]{:T(128)} %get-tuple-element.1229, f32[816]{0:T(1024)S(1)} %reshape.215, s32[816]{0:T(1024)S(1)} %eq.189, f32[816]{0:T(1024)S(1)} %exp.63, f32[816]{0:T(1024)S(1)} %add.404, pred[4096]{0:T(1024)(128)(4,1)S(1)} %iota_compare_fusion.4), kind=kLoop, calls=%fused_computation.33.clone.1 | loop fusion | flops 23396352 | bytes 20071172 | tf_op jit(solution)/shard_map/while/body/eval_jaxpr/convert_element_type | solution.py:134
  323.4 12.1 %select_add_fusion.12 = f32[640,4096]{1,0:T(8,128)} fusion(f32[640,4096]{1,0:T(8,128)} %get-tuple-element.1233, bf16[816,4096]{1,0:T(8,128)(2,1)} %fusion.89, pred[]{:T(512)S(6)} %compare.12, bf16[2,816,640]{2,1,0:T(8,128)(2,1)} %get-tuple-element.1266, s32[]{:T(128)} %get-tuple-element.1229), kind=kOutput, calls=%fused_computation.36.clone.1 | convolution fusion | flops 4283432960 | bytes 28701184 | tf_op jit(solution)/shard_map/while/body/eval_jaxpr/dot_general | solution.py:135
  335.8 8.1 %subtract_multiply_fusion.2 = f32[816,640]{1,0:T(8,128)} fusion(bf16[816,4096]{1,0:T(8,128)(2,1)S(1)} %copy-done, bf16[640,4096]{1,0:T(8,128)(2,1)S(1)} %bitcast.202, bf16[2,816,640]{2,1,0:T(8,128)(2,1)} %get-tuple-element.1266, s32[]{:T(128)} %get-tuple-element.1229), kind=kOutput, calls=%fused_computation.37.clone.1 | convolution fusion | flops 4280279040 | bytes 15060996 | tf_op jit(solution)/shard_map/while/body/eval_jaxpr/dot_general | solution.py:139
  359.4 44.8 %all-reduce.5 = (f32[4096]{0:T(1024)S(1)}, f32[640]{0:T(1024)S(1)}, f32[]{:T(128)}, f32[]{:T(128)}) all-reduce(f32[4096]{0:T(1024)S(1)} %get-tuple-element.406, f32[640]{0:T(1024)S(1)} %get-tuple-element.407, f32[]{:T(128)} %get-tuple-element.408, f32[]{:T(128)S(6)} %convert_element_type.42), channel_id=1, replica_groups=mesh['dp'=8,'rep'=4] {'dp','rep'}, use_global_device_ids=true, to_apply=%region_19.20 | all-reduce | flops 4738 | bytes 37904 | tf_op jit(solution)/shard_map/psum | solution.py:205
  406.7 199.6 %all-reduce.9.cloned.1.call-done = (f32[640,640]{1,0:T(8,128)}, f32[640,640]{1,0:T(8,128)}, f32[640,4096]{1,0:T(8,128)}) async-done(((f32[640,640]{1,0:T(8,128)}, f32[640,640]{1,0:T(8,128)}, f32[640,4096]{1,0:T(8,128)}), (f32[640,640]{1,0:T(8,128)}, f32[640,640]{1,0:T(8,128)}, f32[640,4096]{1,0:T(8,128)})) %all-reduce.9.cloned.1.call-update) | async-done | bytes 13762576 | tf_op jit(solution)/shard_map/psum | solution.py:205
  606.3 7.4 %multiply_reduce_fusion = f32[]{:T(128)} fusion(f32[640,4096]{1,0:T(8,128)} %get-tuple-element.759), kind=kLoop, calls=%fused_computation.83 | loop fusion | flops 5242879 | bytes 10485764 | tf_op jit(solution)/shard_map/reduce_sum | solution.py:194
  619.2 9.7 %broadcast_multiply_fusion = f32[640,4096]{1,0:T(8,128)} fusion(f32[640,4096]{1,0:T(8,128)} %get-tuple-element.759, f32[]{:T(128)S(6)} %rsqrt.3), kind=kLoop, calls=%fused_computation.84 | loop fusion | flops 2621440 | bytes 20971524 | tf_op jit(solution)/shard_map/mul | solution.py:207
  (973 shorter events, 131.0 us)
Async XLA Ops:
  7.2 599.1 %all-reduce.9.cloned.1.call-start = ((), (), s32[]{:S(2)}) async-start(), calls=%async_computation | async-start | bytes 27525120 | tf_op jit(solution)/shard_map/psum | solution.py:205
  11.0 89.7 %copy-start.5 = (s32[64,17,1]{1,0,2:T(8,128)S(1)}, s32[64,17,1]{1,0,2:T(8,128)}, u32[]{:S(2)}) copy-start(s32[64,17,1]{1,0,2:T(8,128)} %fusion.34) | copy-start | bytes 13060
  11.0 115.0 %copy-start.14 = (pred[64,17]{1,0:T(8,128)(4,1)S(1)}, pred[64,17]{1,0:T(8,128)(4,1)}, u32[]{:S(2)}) copy-start(pred[64,17]{1,0:T(8,128)(4,1)} %compare_and_fusion) | copy-start | bytes 3268
  11.0 115.1 %copy-start.6 = (s32[64,17]{1,0:T(8,128)S(1)}, s32[64,17]{1,0:T(8,128)}, u32[]{:S(2)}) copy-start(s32[64,17]{1,0:T(8,128)} %iota_subtract_fusion) | copy-start | bytes 13060
  11.0 115.2 %copy-start.16 = (f32[17]{0:T(128)S(1)}, f32[17]{0:T(128)}, u32[]{:S(2)}) copy-start(f32[17]{0:T(128)} %compare_select_fusion.7) | copy-start | bytes 208
  11.1 115.2 %copy-start.7 = (s32[2]{0:T(128)S(1)}, s32[2]{0:T(128)}, u32[]{:S(2)}) copy-start(s32[2]{0:T(128)} %param.20) | copy-start | bytes 28
  11.1 115.2 %copy-start.10 = (f32[64,2,17]{2,1,0:T(2,128)S(1)}, f32[64,2,17]{2,1,0:T(2,128)}, u32[]{:S(2)}) copy-start(f32[64,2,17]{2,1,0:T(2,128)} %custom-call.20) | copy-start | bytes 26116
  11.1 115.2 %copy-start.11 = (f32[64,2,17]{2,1,0:T(2,128)S(1)}, f32[64,2,17]{2,1,0:T(2,128)}, u32[]{:S(2)}) copy-start(f32[64,2,17]{2,1,0:T(2,128)} %custom-call.21) | copy-start | bytes 26116
  11.1 115.2 %copy-start.12 = (f32[64,2,17]{2,1,0:T(2,128)S(1)}, f32[64,2,17]{2,1,0:T(2,128)}, u32[]{:S(2)}) copy-start(f32[64,2,17]{2,1,0:T(2,128)} %custom-call.22) | copy-start | bytes 26116
  11.1 115.2 %copy-start.13 = (s32[2]{0:T(128)S(1)}, s32[2]{0:T(128)}, u32[]{:S(2)}) copy-start(s32[2]{0:T(128)} %param.19) | copy-start | bytes 28
  11.1 115.2 %copy-start.15 = (f32[2,17]{1,0:T(2,128)S(1)}, f32[2,17]{1,0:T(2,128)}, u32[]{:S(2)}) copy-start(f32[2,17]{1,0:T(2,128)} %custom-call.10) | copy-start | bytes 412
  99.7 134.1 %copy-start.9 = (s32[48,17,1]{1,0,2:T(8,128)S(1)}, s32[48,17,1]{1,0,2:T(8,128)}, u32[]{:S(2)}) copy-start(s32[48,17,1]{1,0,2:T(8,128)} %fusion.37) | copy-start | bytes 9796
  113.2 153.3 %copy-start.4 = (bf16[2,48,640]{2,1,0:T(8,128)(2,1)S(1)}, bf16[2,48,640]{2,1,0:T(8,128)(2,1)}, u32[]{:S(2)}) copy-start(bf16[2,48,640]{2,1,0:T(8,128)(2,1)} %get-tuple-element.1284) | copy-start | bytes 368644
  113.2 153.3 %copy-start.18 = (s32[2,16]{1,0:T(2,128)S(1)}, s32[2,16]{1,0:T(2,128)}, u32[]{:S(2)}) copy-start(s32[2,16]{1,0:T(2,128)} %get-tuple-element.1288) | copy-start | bytes 388
  269.0 21.8 %slice-start.2 = ((s8[5242880]{0:T(1024)(128)(4,1)}), s8[1048576]{0:T(1024)(128)(4,1)S(1)}, s32[]{:S(2)}) async-start(s8[5242880]{0:T(1024)(128)(4,1)} %bitcast.201), calls=%async_computation.3 | async-start | bytes 2097152 | tf_op jit(solution)/shard_map/while
  280.2 10.6 %copy-start = (bf16[816,4096]{1,0:T(8,128)(2,1)S(1)}, bf16[816,4096]{1,0:T(8,128)(2,1)}, u32[]{:S(2)}) copy-start(bf16[816,4096]{1,0:T(8,128)(2,1)} %fusion.89) | copy-start | bytes 20054020 | tf_op jit(solution)/shard_map/while
  280.2 10.6 %slice-start.3 = ((s8[5242880]{0:T(1024)(128)(4,1)}), s8[4194304]{0:T(1024)(128)(4,1)S(1)}, s32[]{:S(2)}) async-start(s8[5242880]{0:T(1024)(128)(4,1)} %bitcast.201), calls=%async_computation.4 | async-start | bytes 8388608 | tf_op jit(solution)/shard_map/while
  299.0 8.8 %slice-start = ((s8[6684672]{0:T(1024)(128)(4,1)}), s8[2490368]{0:T(1024)(128)(4,1)S(1)}, s32[]{:S(2)}) async-start(s8[6684672]{0:T(1024)(128)(4,1)} %bitcast.181), calls=%async_computation.1 | async-start | bytes 4980736 | tf_op jit(solution)/shard_map/while
  312.2 23.3 %slice-start.2 = ((s8[5242880]{0:T(1024)(128)(4,1)}), s8[1048576]{0:T(1024)(128)(4,1)S(1)}, s32[]{:S(2)}) async-start(s8[5242880]{0:T(1024)(128)(4,1)} %bitcast.201), calls=%async_computation.3 | async-start | bytes 2097152 | tf_op jit(solution)/shard_map/while
  323.4 12.1 %copy-start = (bf16[816,4096]{1,0:T(8,128)(2,1)S(1)}, bf16[816,4096]{1,0:T(8,128)(2,1)}, u32[]{:S(2)}) copy-start(bf16[816,4096]{1,0:T(8,128)(2,1)} %fusion.89) | copy-start | bytes 20054020 | tf_op jit(solution)/shard_map/while
  323.4 12.4 %slice-start.3 = ((s8[5242880]{0:T(1024)(128)(4,1)}), s8[4194304]{0:T(1024)(128)(4,1)S(1)}, s32[]{:S(2)}) async-start(s8[5242880]{0:T(1024)(128)(4,1)} %bitcast.201), calls=%async_computation.4 | async-start | bytes 8388608 | tf_op jit(solution)/shard_map/while
  343.9 11.7 %slice-start = ((s8[6684672]{0:T(1024)(128)(4,1)}), s8[2490368]{0:T(1024)(128)(4,1)S(1)}, s32[]{:S(2)}) async-start(s8[6684672]{0:T(1024)(128)(4,1)} %bitcast.181), calls=%async_computation.1 | async-start | bytes 4980736 | tf_op jit(solution)/shard_map/while
  347.0 8.6 %slice-start.1 = ((s8[6684672]{0:T(1024)(128)(4,1)}), s8[4194304]{0:T(1024)(128)(4,1)S(1)}, s32[]{:S(2)}) async-start(s8[6684672]{0:T(1024)(128)(4,1)} %bitcast.181), calls=%async_computation.2 | async-start | bytes 8388608 | tf_op jit(solution)/shard_map/while
  606.3 7.4 %copy-start.3 = (f32[640,640]{1,0:T(8,128)S(1)}, f32[640,640]{1,0:T(8,128)}, u32[]{:S(2)}) copy-start(f32[640,640]{1,0:T(8,128)} %get-tuple-element.758) | copy-start | bytes 4915204
  (7 other events, 33.2 us)
Sparse Core Ops, SparseCore 0:
  357.6 248.6 all-reduce.8
where the time goes:
time: 649 us; the launch traced here: 640 us
  waiting for transfers between devices  200 us (31%)
  local copies, waits for them, and re-layouts  149 us (23%)
  other arithmetic  109 us (17%)
  matrix products  68.8 us (11%)
  loops' own time  47.9 us (7%)
  blocking collectives  44.8 us (7%)
  between operations  21.2 us (3%)
    psum x1, waiting for transfers between devices, per_device(): lax.psum((grads[0], grads[1], grads[2], grads[3], grads[4]), ('dp', 'rep'))  200 us
    another operation x1, loops' own time, lattice(): lax.scan(both_ways, (first_diag, neg_grid), inputs)  46.1 us
    psum x1, blocking collectives, per_device(): lax.psum((grads[0], grads[1], grads[2], grads[3], grads[4]), ('dp', 'rep'))  44.8 us
    dynamic_slice x256, local copies, waits for them, and re-layouts, lattice(): lax.scan(both_ways, (first_diag, neg_grid), inputs)  39.8 us
    gather x9, local copies, waits for them, and re-layouts, unskewed(): by_utterance[:, frame_ids[:, None] + positions[None, :], positions[None, :]]  30.5 us
    reduce_sum x2, other arithmetic, joint_forward(): jnp.sum(jnp.where(is_target, log_probs, 0.0), axis=1)  25.4 us
    gather x6, local copies, waits for them, and re-layouts, skewed(): grid[:, jnp.clip(frame_index, 0, num_frames - 1), positions[None, :]]  25.2 us
    dynamic_update_slice x6, local copies, waits for them, and re-layouts, local_sums(): lax.scan(forward_one, None, (enc, pred, labels))  24.7 us
  transfers between devices with their start and end apart: 1, of which 1 were waited for; matrix products, arithmetic and copies ran while one was open for 0% of the time, Pallas kernels for 0%

commit v1 on v0

--- a/solution.py
+++ b/solution.py
@@ -202,7 +202,8 @@
     count_local = jnp.sum(label_len).astype(jnp.float32)
     param_count = jnp.float32(w_enc.size + w_pred.size + w_out.size + b_out.size + b_joint.size)
     loss_total, label_total = lax.psum((loss_local, count_local), ("dp", "rep"))
-    summed = lax.psum((grads[0], grads[1], grads[2], grads[3], grads[4]), ("dp", "rep"))
+    half = lax.psum((grads[0], grads[1], grads[2], grads[3], grads[4]), "rep")
+    summed = lax.psum(half, "dp")
     scale = lax.rsqrt(squares(summed) / param_count + EPS)
     result = tuple((item * scale for item in summed))
     return (result[0], result[1], result[2], result[3], result[4], loss_total / label_total)

time: 649 us -> 1080 us (1.66)
  waiting for transfers between devices: 200 us -> 576 us
  blocking collectives: 44.8 us -> 96.2 us
    psum x1 -> x2, waiting for transfers between devices: 200 us -> 576 us  [the longest x1 333 us: per_device(): summed = lax.psum(half, 'dp')]
    psum x1 -> x3, blocking collectives: 44.8 us -> 96.2 us  [the longest x1 44.4 us: per_device(): loss_total, label_total = lax.psum((loss_local, count_local), ('dp', 'rep'))]
  transfers between devices with their start and end apart: 1 -> 2, of which waited for: 1 -> 2; matrix products, arithmetic and copies ran while one was open for 0% -> 0% of each run, Pallas kernels for 0% -> 0%
where the time goes in v1:
time: 1080 us; the launch traced here: 1070 us
  waiting for transfers between devices  576 us (53%)
  local copies, waits for them, and re-layouts  149 us (14%)
  other arithmetic  109 us (10%)
  blocking collectives  96.2 us (9%)
  matrix products  68.8 us (6%)
  loops' own time  48.1 us (4%)
  between operations  21.3 us (2%)
    psum x1, waiting for transfers between devices, per_device(): summed = lax.psum(half, 'dp')  333 us
    psum x1, waiting for transfers between devices, per_device(): half = lax.psum((grads[0], grads[1], grads[2], grads[3], grads[4]), 'rep')  243 us
    another operation x1, loops' own time, lattice(): lax.scan(both_ways, (first_diag, neg_grid), inputs)  46.1 us
    psum x1, blocking collectives, per_device(): loss_total, label_total = lax.psum((loss_local, count_local), ('dp', 'rep'))  44.4 us
    psum x1, blocking collectives, per_device(): summed = lax.psum(half, 'dp')  40.5 us
    dynamic_slice x256, local copies, waits for them, and re-layouts, lattice(): lax.scan(both_ways, (first_diag, neg_grid), inputs)  39.8 us
    gather x9, local copies, waits for them, and re-layouts, unskewed(): by_utterance[:, frame_ids[:, None] + positions[None, :], positions[None, :]]  30.3 us
    reduce_sum x2, other arithmetic, joint_forward(): jnp.sum(jnp.where(is_target, log_probs, 0.0), axis=1)  25.4 us
  transfers between devices with their start and end apart: 2, of which 2 were waited for; matrix products, arithmetic and copies ran while one was open for 0% of the time, Pallas kernels for 0%

profile of v1, /device:TPU:0, one launch (start us, length us, event | category | flops | bytes accessed | tf_op | source)
XLA Modules:
  0.0 1067.3 jit_solution(571260400173169778)
XLA Ops:
  11.1 88.6 %while.58 = (s32[]{:T(128)}, bf16[2,816,640]{2,1,0:T(8,128)(2,1)}, f32[2,816,4096]{2,1,0:T(8,128)}, f32[2,48,17]{2,1,0:T(8,128)S(1)}, f32[2,48,17]{2,1,0:T(8,128...) while((s32[]{:T(128)}, bf16[2,816,640]{2,1,0:T(8,128)(2,1)}, ...), condition=%wide.region_4.5_spmd, body=%wide.region_0.4_spmd.sunk | while | flops 4369261056 | bytes 147507888 | solution.py:167
  28.9 12.7 %select_reduce_fusion.2 = (f32[816]{0:T(1024)S(1)}, f32[816,4096]{1,0:T(8,128)}) fusion(s32[816]{0:T(1024)S(1)} %eq.178, f32[816]{0:T(1024)S(1)} %log.11, f32[816]{0:T(1024)S(1)} %get-tuple-element.1058, f32[816,4096]{1,0:T(8,128)} %copy-done.1, f32[4096]{0:T(1024)S(1)} %convert_element_type.65), kind=kLoop, calls=%fused_computation.62.clone.1 | loop fusion | flops 20053200 | bytes 26768128 | tf_op jit(solution)/shard_map/while/body/eval_jaxpr/reduce_sum | solution.py:110
  43.1 11.3 %bitcast_dynamic-update-slice_fusion.5 = f32[2,816,4096]{2,1,0:T(8,128)} fusion(f32[2,816,4096]{2,1,0:T(8,128)} %get-tuple-element.1125, s32[]{:T(128)} %get-tuple-element.1123, f32[816,4096]{1,0:T(8,128)} %get-tuple-element.1059), kind=kLoop, calls=%fused_computation.61.clone.1 | loop fusion | bytes 26739200 | tf_op jit(solution)/shard_map/while/body/jit(dynamic_update_index_in_dim)/dynamic_update_slice | solution.py:167
  73.2 12.7 %select_reduce_fusion.2 = (f32[816]{0:T(1024)S(1)}, f32[816,4096]{1,0:T(8,128)}) fusion(s32[816]{0:T(1024)S(1)} %eq.178, f32[816]{0:T(1024)S(1)} %log.11, f32[816]{0:T(1024)S(1)} %get-tuple-element.1058, f32[816,4096]{1,0:T(8,128)} %copy-done.1, f32[4096]{0:T(1024)S(1)} %convert_element_type.65), kind=kLoop, calls=%fused_computation.62.clone.1 | loop fusion | flops 20053200 | bytes 26768128 | tf_op jit(solution)/shard_map/while/body/eval_jaxpr/reduce_sum | solution.py:110
  87.3 11.3 %bitcast_dynamic-update-slice_fusion.5 = f32[2,816,4096]{2,1,0:T(8,128)} fusion(f32[2,816,4096]{2,1,0:T(8,128)} %get-tuple-element.1125, s32[]{:T(128)} %get-tuple-element.1123, f32[816,4096]{1,0:T(8,128)} %get-tuple-element.1059), kind=kLoop, calls=%fused_computation.61.clone.1 | loop fusion | bytes 26739200 | tf_op jit(solution)/shard_map/while/body/jit(dynamic_update_index_in_dim)/dynamic_update_slice | solution.py:167
  100.8 12.3 %gather_fusion = f32[1088,2]{1,0:T(8,128)S(1)} fusion(f32[2,48,17]{0,1,2:T(8,128)S(1)} %copy.55, s32[1088]{0:T(1024)S(1)} %reshape.180), kind=kCustom, calls=%fused_computation | custom fusion | bytes 26112 | tf_op jit(solution)/shard_map/gather | solution.py:21
  113.6 12.1 %gather_fusion.1 = f32[1088,2]{1,0:T(8,128)S(1)} fusion(f32[2,48,17]{0,1,2:T(8,128)S(1)} %copy.57, s32[1088]{0:T(1024)S(1)} %reshape.180), kind=kCustom, calls=%fused_computation.1 | custom fusion | bytes 26112 | tf_op jit(solution)/shard_map/gather | solution.py:21
  126.3 106.5 %while.59 = (s32[]{:T(128)}, f32[2,17]{1,0:T(2,128)S(1)}, f32[2,17]{1,0:T(2,128)S(1)}, f32[64,2,17]{2,1,0:T(2,128)S(1)}, f32[64,2,17]{2,1,0:T(2,128)S(1)}, /*ind...) while((s32[]{:T(128)}, f32[2,17]{1,0:T(2,128)S(1)}, ...), condition=%wide.region_6.7_spmd.clone, body=%wide.region_5.6_spmd.clone.sunk | while | flops 1434 | bytes 22799 | solution.py:84
  233.9 9.8 gather_fusion.2
  245.2 9.8 gather_fusion.4
  256.0 9.8 gather_fusion.3
  266.2 91.1 %while.60 = (s32[]{:T(128)}, f32[]{:T(128)}, f32[640,640]{1,0:T(8,128)}, f32[640,640]{1,0:T(8,128)}, f32[640,4096]{1,0:T(8,128)}, /*index=5*/f32[4096]{0:T(1024)...) while((s32[]{:T(128)}, f32[]{:T(128)}, ...), condition=%wide.region_12.13_spmd.clone, body=%wide.region_7.12_spmd.clone.sunk | while | flops 8649718784 | bytes 146314000 | solution.py:183
  269.0 11.2 %fusion.89 = bf16[816,4096]{1,0:T(8,128)(2,1)} fusion(f32[2,816,4096]{2,1,0:T(8,128)} %get-tuple-element.1264, s32[]{:T(128)} %get-tuple-element.1234, f32[816]{0:T(1024)S(1)} %reshape.215, s32[816]{0:T(1024)S(1)} %eq.189, f32[816]{0:T(1024)S(1)} %exp.63, f32[816]{0:T(1024)S(1)} %add.414, pred[4096]{0:T(1024)(128)(4,1)S(1)} %iota_compare_fusion.4), kind=kLoop, calls=%fused_computation.33.clone.1 | loop fusion | flops 23396352 | bytes 20071172 | tf_op jit(solution)/shard_map/while/body/eval_jaxpr/convert_element_type | solution.py:134
  280.2 10.6 select_add_fusion.12
  290.8 8.1 subtract_multiply_fusion.2
  312.2 11.2 %fusion.89 = bf16[816,4096]{1,0:T(8,128)(2,1)} fusion(f32[2,816,4096]{2,1,0:T(8,128)} %get-tuple-element.1264, s32[]{:T(128)} %get-tuple-element.1234, f32[816]{0:T(1024)S(1)} %reshape.215, s32[816]{0:T(1024)S(1)} %eq.189, f32[816]{0:T(1024)S(1)} %exp.63, f32[816]{0:T(1024)S(1)} %add.414, pred[4096]{0:T(1024)(128)(4,1)S(1)} %iota_compare_fusion.4), kind=kLoop, calls=%fused_computation.33.clone.1 | loop fusion | flops 23396352 | bytes 20071172 | tf_op jit(solution)/shard_map/while/body/eval_jaxpr/convert_element_type | solution.py:134
  323.4 12.1 %select_add_fusion.12 = f32[640,4096]{1,0:T(8,128)} fusion(f32[640,4096]{1,0:T(8,128)} %get-tuple-element.1238, bf16[816,4096]{1,0:T(8,128)(2,1)} %fusion.89, pred[]{:T(512)S(6)} %compare.12, bf16[2,816,640]{2,1,0:T(8,128)(2,1)} %get-tuple-element.1271, s32[]{:T(128)} %get-tuple-element.1234), kind=kOutput, calls=%fused_computation.36.clone.1 | convolution fusion | flops 4283432960 | bytes 28701184 | tf_op jit(solution)/shard_map/while/body/eval_jaxpr/dot_general | solution.py:135
  335.8 8.1 subtract_multiply_fusion.2
  357.5 242.6 %all-reduce.15.cloned.1.call-done = (f32[640,640]{1,0:T(8,128)}, f32[640,640]{1,0:T(8,128)}, f32[640,4096]{1,0:T(8,128)}) async-done(((f32[640,640]{1,0:T(8,128)}, f32[640,640]{1,0:T(8,128)}, f32[640,4096]{1,0:T(8,128)}), (f32[640,640]{1,0:T(8,128)}, f32[640,640]{1,0:T(8,128)}, f32[640,4096]{1,0:T(8,128)})) %all-reduce.15.cloned.1.call-update) | async-done | bytes 13762576 | tf_op jit(solution)/shard_map/psum | solution.py:205
  602.0 44.4 %all-reduce.5 = (f32[]{:T(128)}, f32[]{:T(128)}) all-reduce(f32[]{:T(128)} %get-tuple-element.408, f32[]{:T(128)S(6)} %convert_element_type.42), channel_id=1, replica_groups=mesh['dp'=8,'rep'=4] {'dp','rep'}, use_global_device_ids=true, to_apply=%region_28.29 | all-reduce | flops 2 | bytes 16 | tf_op jit(solution)/shard_map/psum | solution.py:204
  647.8 11.3 %all-reduce.8 = (f32[4096]{0:T(1024)S(1)}, f32[640]{0:T(1024)S(1)}) all-reduce(f32[4096]{0:T(1024)S(1)} %get-tuple-element.406, f32[640]{0:T(1024)S(1)} %get-tuple-element.407), channel_id=1, replica_groups=mesh['dp'=8,'rep'=4] {'rep'}, use_global_device_ids=true, to_apply=%region_22.23 | all-reduce | flops 4736 | bytes 37888 | tf_op jit(solution)/shard_map/psum | solution.py:205
  659.1 40.5 %all-reduce.6 = (f32[4096]{0:T(1024)S(1)}, f32[640]{0:T(1024)S(1)}) all-reduce(f32[4096]{0:T(1024)S(1)} %get-tuple-element.760, f32[640]{0:T(1024)S(1)} %get-tuple-element.761), channel_id=1, replica_groups=mesh['dp'=8,'rep'=4] {'dp'}, use_global_device_ids=true, to_apply=%region_23.24 | all-reduce | flops 4736 | bytes 37888 | tf_op jit(solution)/shard_map/psum | solution.py:206
  700.7 333.0 %all-reduce.13.cloned.1.call-done = (f32[640,640]{1,0:T(8,128)}, f32[640,640]{1,0:T(8,128)}, f32[640,4096]{1,0:T(8,128)}) async-done(((f32[640,640]{1,0:T(8,128)}, f32[640,640]{1,0:T(8,128)}, f32[640,4096]{1,0:T(8,128)}), (f32[640,640]{1,0:T(8,128)}, f32[640,640]{1,0:T(8,128)}, f32[640,4096]{1,0:T(8,128)})) %all-reduce.13.cloned.1.call-update) | async-done | bytes 13762576 | tf_op jit(solution)/shard_map/psum | solution.py:206
  1046.6 9.7 broadcast_multiply_fusion
  (978 shorter events, 153.4 us)
Async XLA Ops:
  7.2 592.9 %all-reduce.15.cloned.1.call-start = ((), (), s32[]{:S(2)}) async-start(), calls=%async_computation.1 | async-start | bytes 27525120 | tf_op jit(solution)/shard_map/psum | solution.py:205
  11.0 89.7 %copy-start.5 = (s32[64,17,1]{1,0,2:T(8,128)S(1)}, s32[64,17,1]{1,0,2:T(8,128)}, u32[]{:S(2)}) copy-start(s32[64,17,1]{1,0,2:T(8,128)} %fusion.34) | copy-start | bytes 13060
  11.0 115.0 %copy-start.14 = (pred[64,17]{1,0:T(8,128)(4,1)S(1)}, pred[64,17]{1,0:T(8,128)(4,1)}, u32[]{:S(2)}) copy-start(pred[64,17]{1,0:T(8,128)(4,1)} %compare_and_fusion) | copy-start | bytes 3268
  11.0 115.1 %copy-start.6 = (s32[64,17]{1,0:T(8,128)S(1)}, s32[64,17]{1,0:T(8,128)}, u32[]{:S(2)}) copy-start(s32[64,17]{1,0:T(8,128)} %iota_subtract_fusion) | copy-start | bytes 13060
  11.0 115.2 %copy-start.16 = (f32[17]{0:T(128)S(1)}, f32[17]{0:T(128)}, u32[]{:S(2)}) copy-start(f32[17]{0:T(128)} %compare_select_fusion.7) | copy-start | bytes 208
  11.1 115.2 %copy-start.7 = (s32[2]{0:T(128)S(1)}, s32[2]{0:T(128)}, u32[]{:S(2)}) copy-start(s32[2]{0:T(128)} %param.20) | copy-start | bytes 28
  11.1 115.2 %copy-start.10 = (f32[64,2,17]{2,1,0:T(2,128)S(1)}, f32[64,2,17]{2,1,0:T(2,128)}, u32[]{:S(2)}) copy-start(f32[64,2,17]{2,1,0:T(2,128)} %custom-call.20) | copy-start | bytes 26116
  11.1 115.2 %copy-start.11 = (f32[64,2,17]{2,1,0:T(2,128)S(1)}, f32[64,2,17]{2,1,0:T(2,128)}, u32[]{:S(2)}) copy-start(f32[64,2,17]{2,1,0:T(2,128)} %custom-call.21) | copy-start | bytes 26116
  11.1 115.2 %copy-start.12 = (f32[64,2,17]{2,1,0:T(2,128)S(1)}, f32[64,2,17]{2,1,0:T(2,128)}, u32[]{:S(2)}) copy-start(f32[64,2,17]{2,1,0:T(2,128)} %custom-call.22) | copy-start | bytes 26116
  11.1 115.2 %copy-start.13 = (s32[2]{0:T(128)S(1)}, s32[2]{0:T(128)}, u32[]{:S(2)}) copy-start(s32[2]{0:T(128)} %param.19) | copy-start | bytes 28
  11.1 115.2 %copy-start.15 = (f32[2,17]{1,0:T(2,128)S(1)}, f32[2,17]{1,0:T(2,128)}, u32[]{:S(2)}) copy-start(f32[2,17]{1,0:T(2,128)} %custom-call.10) | copy-start | bytes 412
  99.7 134.1 %copy-start.9 = (s32[48,17,1]{1,0,2:T(8,128)S(1)}, s32[48,17,1]{1,0,2:T(8,128)}, u32[]{:S(2)}) copy-start(s32[48,17,1]{1,0,2:T(8,128)} %fusion.37) | copy-start | bytes 9796
  113.2 153.1 %copy-start.4 = (bf16[2,48,640]{2,1,0:T(8,128)(2,1)S(1)}, bf16[2,48,640]{2,1,0:T(8,128)(2,1)}, u32[]{:S(2)}) copy-start(bf16[2,48,640]{2,1,0:T(8,128)(2,1)} %get-tuple-element.1299) | copy-start | bytes 368644
  113.2 153.1 %copy-start.18 = (s32[2,16]{1,0:T(2,128)S(1)}, s32[2,16]{1,0:T(2,128)}, u32[]{:S(2)}) copy-start(s32[2,16]{1,0:T(2,128)} %get-tuple-element.1307) | copy-start | bytes 388
  269.0 21.8 %slice-start.2 = ((s8[5242880]{0:T(1024)(128)(4,1)}), s8[1048576]{0:T(1024)(128)(4,1)S(1)}, s32[]{:S(2)}) async-start(s8[5242880]{0:T(1024)(128)(4,1)} %bitcast.201), calls=%async_computation.4 | async-start | bytes 2097152 | tf_op jit(solution)/shard_map/while
  280.2 10.6 copy-start
  280.2 10.6 slice-start.3
  299.0 8.8 slice-start
  312.2 23.3 %slice-start.2 = ((s8[5242880]{0:T(1024)(128)(4,1)}), s8[1048576]{0:T(1024)(128)(4,1)S(1)}, s32[]{:S(2)}) async-start(s8[5242880]{0:T(1024)(128)(4,1)} %bitcast.201), calls=%async_computation.4 | async-start | bytes 2097152 | tf_op jit(solution)/shard_map/while
  323.4 12.1 %copy-start = (bf16[816,4096]{1,0:T(8,128)(2,1)S(1)}, bf16[816,4096]{1,0:T(8,128)(2,1)}, u32[]{:S(2)}) copy-start(bf16[816,4096]{1,0:T(8,128)(2,1)} %fusion.89) | copy-start | bytes 20054020 | tf_op jit(solution)/shard_map/while
  323.4 12.4 %slice-start.3 = ((s8[5242880]{0:T(1024)(128)(4,1)}), s8[4194304]{0:T(1024)(128)(4,1)S(1)}, s32[]{:S(2)}) async-start(s8[5242880]{0:T(1024)(128)(4,1)} %bitcast.201), calls=%async_computation.5 | async-start | bytes 8388608 | tf_op jit(solution)/shard_map/while
  343.9 11.7 %slice-start = ((s8[6684672]{0:T(1024)(128)(4,1)}), s8[2490368]{0:T(1024)(128)(4,1)S(1)}, s32[]{:S(2)}) async-start(s8[6684672]{0:T(1024)(128)(4,1)} %bitcast.181), calls=%async_computation.2 | async-start | bytes 4980736 | tf_op jit(solution)/shard_map/while
  347.0 8.6 slice-start.1
  357.4 676.3 %all-reduce.13.cloned.1.call-start = ((), (), s32[]{:S(2)}) async-start(), calls=%async_computation | async-start | bytes 27525120 | tf_op jit(solution)/shard_map/psum | solution.py:206
  (8 other events, 40.6 us)
Sparse Core Ops, SparseCore 0:
  357.5 242.4 all-reduce.14
  604.8 428.8 all-reduce.12
